TPU v7x, 32 devices: a whole 2x2x4 slice. The times are simulated.
32 devices in a mesh: chan: 8 (over z, y), bins: 4 (over x, core).
Axes of the slice: x: 2, y: 2, z: 4, core: 2. Of those that a mesh axis runs over, the one named last changes fastest.
Arguments:
- effects: bfloat16 [64, 8192, 256], P('chan', 'bins'), may hold values from -0.19921875 to 0.19921875
- nominal: float32 [64, 8192], P('chan', 'bins'), may hold values from 0.2 to 5
- observed: int32 [64, 8192], P('chan', 'bins'), may hold values from 0 to 7
- mc_variance: float32 [64, 8192], P('chan', 'bins'), may hold values from 0.002 to 0.5
- theta: float32 [8192], replicated, may hold values from -4 to 4
- nuisance_index: int32 [64, 256], replicated, may hold values from 0 to 8191, as said below
- bin_counts: int32 [64], P('chan'), may hold values from 1 to 8192, 262144 in all
- tile_owner: int32 [256], replicated, may hold values from 0 to 255, each once
Outputs:
- hessian_tiles: float32 [256, 512, 512], P(('chan', 'bins'))
- gradient: float32 [8192], P(('chan', 'bins'))
Inputs may be any that keep to these rules, and one draw needn't show every extreme that they name: `nuisance_index`: each channel's list is 2 runs of 128 consecutive nuisances, each run starting at a multiple of 128, the runs distinct and in increasing order. Bins at positions bin_counts[c] and beyond of channel c carry no data. `tile_owner`: every tile number appears exactly once.
All inputs are finite; a program needn't handle non-finite values. No bound on the sum of `bin_counts` on one device may be relied on, other than what follows from the above.
Results may differ from a plain program's by a relative error of at most 0.0029.
Values sent between devices are 32-bit elements; how exact they have to be, the bound alone decides.
A program may use at most 128 MiB of HBM per device.

v0:
```python
import functools

import jax
import jax.numpy as jnp
from jax import lax
from jax.experimental import pallas as pl
from jax.experimental.pallas import tpu as pltpu
from jax.sharding import PartitionSpec as P

GW = 128
TILE = 512
EXTRA = 8


def channel_payload(eff, chosen, nominal, observed, variance, live):
    eff_t = eff.T
    exponent = jnp.dot(chosen, eff_t, preferred_element_type=jnp.float32)[0:8]
    expected = nominal * jnp.exp(exponent)
    denominator = 1.0 + expected * variance
    residual = jnp.where(live, (expected - observed) / denominator, 0.0)
    weight = jnp.where(live, expected / denominator, 0.0)
    weighted = (eff_t.astype(jnp.float32) * weight[0:1]).astype(jnp.bfloat16)
    residual_rows = jnp.concatenate([residual, residual], axis=0).astype(jnp.bfloat16)
    left = jnp.concatenate([weighted, residual_rows], axis=0)
    full = jnp.dot(left, eff, preferred_element_type=jnp.float32)
    first, off, second = full[:GW, :GW], full[:GW, GW:], full[GW : 2 * GW, GW:]
    row = lax.broadcasted_iota(jnp.int32, (GW, GW), 0)
    col = lax.broadcasted_iota(jnp.int32, (GW, GW), 1)
    packed = jnp.where(row <= col, first, second)
    second_diag = jnp.sum(jnp.where(row == col, second, 0.0), axis=0, keepdims=True)
    grad0 = full[2 * GW : 2 * GW + 8, :GW]
    grad1 = full[2 * GW : 2 * GW + 8, GW:]
    which = lax.broadcasted_iota(jnp.int32, (EXTRA, GW), 0)
    extra = jnp.where(
        which == 0, grad0, jnp.where(which == 1, grad1, jnp.broadcast_to(second_diag, (EXTRA, GW)))
    )
    return packed, off, extra


def curvature_kernel(groups_ref, counts_ref, eff_ref, nom_ref, obs_ref, var_ref, theta_ref, out_ref):
    chan = lax.axis_index("chan")
    bins = lax.axis_index("bins")
    c = pl.program_id(0)
    size = eff_ref.shape[1]
    base = chan * pl.num_programs(0) + c
    g0, g1 = groups_ref[base, 0], groups_ref[base, 1]
    chosen = jnp.concatenate([theta_ref[g0], theta_ref[g1]], axis=1).astype(jnp.bfloat16)
    chosen = jnp.broadcast_to(chosen, (16, 2 * GW))
    line = pl.ds(c, 1)
    nominal, observed, variance = nom_ref[line], obs_ref[line].astype(jnp.float32), var_ref[line]
    position = bins * size + lax.broadcasted_iota(jnp.int32, (8, size), 1)
    packed, off, extra = channel_payload(
        eff_ref[0], chosen, nominal, observed, variance, position < counts_ref[c]
    )
    out_ref[0, :GW] = packed
    out_ref[0, GW : 2 * GW] = off
    out_ref[0, 2 * GW :] = extra


def curvature(effects, nominal, observed, variance, theta, groups, counts):
    chans, size, width = effects.shape
    rows = 2 * GW + EXTRA
    whole = lambda *shape: pl.BlockSpec(shape, lambda c, *_: (0,) * len(shape))
    return pl.pallas_call(
        curvature_kernel,
        grid_spec=pltpu.PrefetchScalarGridSpec(
            num_scalar_prefetch=2,
            grid=(chans,),
            in_specs=[
                pl.BlockSpec((1, size, width), lambda c, *_: (c, 0, 0)),
                whole(chans, size),
                whole(chans, size),
                whole(chans, size),
                whole(theta.shape[0] // GW, 1, GW),
            ],
            out_specs=pl.BlockSpec((1, rows, GW), lambda c, *_: (c, 0, 0)),
        ),
        out_shape=jax.ShapeDtypeStruct((chans, rows, GW), jnp.float32),
        compiler_params=pltpu.CompilerParams(vmem_limit_bytes=58 * 2**20),
        name="curvature",
    )(
        groups,
        counts,
        effects,
        nominal,
        observed,
        variance,
        theta.reshape(-1, 1, GW),
    )


def place_kernel(
    groups_ref, owner_ref, payload_ref, theta_ref, tiles_ref, grad_ref,
    lookup, entries, counts,
):
    step = pl.program_id(0)
    slots = counts.shape[0] - 1
    device = lax.axis_index("chan") * lax.axis_size("bins") + lax.axis_index("bins")
    chans = payload_ref.shape[0]
    per_tile = TILE // GW
    total_groups = theta_ref.shape[0]
    side = total_groups // per_tile
    shift = per_tile.bit_length() - 1
    room = 4 * chans
    start = device * slots

    @pl.when(step == 0)
    def _():
        def clear(i, _):
            for j in range(16):
                lookup[i * 16 + j] = slots
            return 0

        lax.fori_loop(0, side * side // 16, clear, 0)
        counts[slots] = 0
        for s in range(slots):
            counts[s] = 0
            lookup[owner_ref[start + s]] = s

        def visit(pair, _):
            for c in (pair * 2, pair * 2 + 1):
                a, b = groups_ref[c, 0], groups_ref[c, 1]
                ta, tb = a >> shift, b >> shift
                ra, rb = a & (per_tile - 1), b & (per_tile - 1)
                cases = ((ta, ta, ra, ra), (tb, tb, rb, rb), (ta, tb, ra, rb), (tb, ta, rb, ra))
                for kind, (tr, tc, rr, rc) in enumerate(cases):
                    slot = lookup[tr * side + tc]
                    n = counts[slot]
                    entries[slot * room + n] = ((((c << shift) + rr) << shift) + rc) * 4 + kind
                    counts[slot] = n + 1
            return 0

        lax.fori_loop(0, chans // 2, visit, 0)

    tile = owner_ref[start + step]

    tiles_ref[...] = jnp.zeros_like(tiles_ref)
    eye = (
        lax.broadcasted_iota(jnp.int32, (GW, GW), 0) == lax.broadcasted_iota(jnp.int32, (GW, GW), 1)
    ).astype(jnp.float32)

    @pl.when(tile // side == tile % side)
    def _():
        for r in range(per_tile):
            tiles_ref[0, r * GW : (r + 1) * GW, r * GW : (r + 1) * GW] = eye

    row = lax.broadcasted_iota(jnp.int32, (GW, GW), 0)
    col = lax.broadcasted_iota(jnp.int32, (GW, GW), 1)

    def accumulate(i, _):
        code = entries[step * room + i]
        kind = code & 3
        rc = (code >> 2) & (per_tile - 1)
        rr = (code >> (2 + shift)) & (per_tile - 1)
        c = code >> (2 + 2 * shift)
        at = (
            0,
            pl.ds(pl.multiple_of(rr * GW, GW), GW),
            pl.ds(pl.multiple_of(rc * GW, GW), GW),
        )

        @pl.when(kind == 0)
        def _():
            upper = jnp.where(row <= col, payload_ref[c, :GW], 0.0)
            tiles_ref[at] += upper + jnp.where(row > col, upper.T, 0.0)

        @pl.when(kind == 1)
        def _():
            lower = jnp.where(row > col, payload_ref[c, :GW], 0.0)
            diag = jnp.where(row == col, payload_ref[c, 2 * GW + 2 : 2 * GW + 3], 0.0)
            tiles_ref[at] += lower + lower.T + diag

        @pl.when(kind == 2)
        def _():
            tiles_ref[at] += payload_ref[c, GW : 2 * GW]

        @pl.when(kind == 3)
        def _():
            tiles_ref[at] += payload_ref[c, GW : 2 * GW].T

        return 0

    lax.fori_loop(0, counts[step], accumulate, 0)

    @pl.when(step == slots - 1)
    def _():
        mine = grad_ref.shape[0]
        first = device * total_groups // (lax.axis_size("chan") * lax.axis_size("bins"))
        for m in range(mine):
            grad_ref[m] = theta_ref[first + m]

        def add(c, _):
            for r in range(2):
                m = groups_ref[c, r] - first

                @pl.when(jnp.logical_and(m >= 0, m < mine))
                def _(m=m, r=r):
                    grad_ref[m] += payload_ref[c, 2 * GW + r : 2 * GW + r + 1]

            return 0

        lax.fori_loop(0, chans, add, 0)


def place(payload, theta, groups, tile_owner, slots, mine):
    chans, rows = payload.shape[:2]
    return pl.pallas_call(
        place_kernel,
        grid_spec=pltpu.PrefetchScalarGridSpec(
            num_scalar_prefetch=2,
            grid=(slots,),
            in_specs=[
                pl.BlockSpec(memory_space=pltpu.VMEM),
                pl.BlockSpec((theta.shape[0] // GW, 1, GW), lambda s, *_: (0, 0, 0)),
            ],
            out_specs=[
                pl.BlockSpec((1, TILE, TILE), lambda s, *_: (s, 0, 0)),
                pl.BlockSpec((mine, 1, GW), lambda s, *_: (0, 0, 0)),
            ],
            scratch_shapes=[
                pltpu.SMEM((tile_owner.shape[0],), jnp.int32),
                pltpu.SMEM(((slots + 1) * chans * 4,), jnp.int32),
                pltpu.SMEM((slots + 1,), jnp.int32),
            ],
        ),
        out_shape=[
            jax.ShapeDtypeStruct((slots, TILE, TILE), jnp.float32),
            jax.ShapeDtypeStruct((mine, 1, GW), jnp.float32),
        ],
        compiler_params=pltpu.CompilerParams(
            vmem_limit_bytes=4 * chans * (rows + EXTRA) * GW + 8 * 2**20
        ),
        name="place",
    )(groups, tile_owner, payload, theta.reshape(-1, 1, GW))


COLORS = ((0, 104, "zxy"), (104, 104, "zyx"), (208, 56, "xyz"))
DEEP = 4


def exchange_kernel(
    ydim, groups_ref, counts_ref, eff_ref, nom_ref, obs_ref, var_ref, theta_ref, out_ref,
    eff_held, parts_ref, swap, cross, total, eff_sem, swap_recv, cross_recv, recv, drecv, send,
):
    chan, bins = lax.axis_index("chan"), lax.axis_index("bins")
    zdim = lax.axis_size("chan") // ydim
    nbins = lax.axis_size("bins")
    z, y = chan // ydim, chan % ydim
    x, core = bins // 2, bins % 2
    held = parts_ref.shape[0] // nbins
    issued = []

    def device(zz, yy, xx, kk):
        return {"chan": zz * ydim + yy, "bins": xx * 2 + kk}

    def copy(src, dst, recv_sem, target, cond=None):
        made = pltpu.make_async_remote_copy(
            src_ref=src,
            dst_ref=dst,
            send_sem=send.at[len(issued)],
            recv_sem=recv_sem,
            device_id=target,
            device_id_type=pl.DeviceIdType.MESH,
        )
        issued.append((made, cond))
        run(cond, made.start)

    def run(cond, action):
        if cond is None:
            action()
        else:
            pl.when(cond)(action)

    partner = device(z, y, x, 1 - core)
    beside = device(z, y, 1 - x, core)
    below_there, above_there = z > 0, z < zdim - 1

    barrier = pltpu.get_barrier_semaphore()
    for target, cond in (
        (partner, None),
        (beside, None),
        (device(z, 1 - y, x, core), None),
        (device(z - 1, y, x, core), below_there),
        (device(z + 1, y, x, core), above_there),
    ):
        run(cond, lambda target=target: pl.semaphore_signal(
            barrier, 1, device_id=target, device_id_type=pl.DeviceIdType.MESH
        ))
    far, near = (1 - x) * 2, x * 2
    owners = (far + 1 - core, far + core, near + 1 - core, near + core)
    size = eff_ref.shape[1]

    def load(q, i):
        at = q * held + i
        return pltpu.make_async_copy(eff_ref.at[owners[q] * held + i], eff_held.at[at], eff_sem.at[at])

    for q in range(4):
        for i in range(held):
            load(q, i).start()

    def compute(q):
        for i in range(held):
            load(q, i).wait()

        def one(i, _):
            c = owners[q] * held + i
            base = chan * nbins * held + c
            g0, g1 = groups_ref[base, 0], groups_ref[base, 1]
            chosen = jnp.concatenate([theta_ref[g0], theta_ref[g1]], axis=1).astype(jnp.bfloat16)
            chosen = jnp.broadcast_to(chosen, (16, 2 * GW))
            line = pl.ds(c, 1)
            position = bins * size + lax.broadcasted_iota(jnp.int32, (8, size), 1)
            packed, off, extra = channel_payload(
                eff_held[q * held + i],
                chosen,
                nom_ref[line],
                obs_ref[line].astype(jnp.float32),
                var_ref[line],
                position < counts_ref[c],
            )
            parts_ref[q * held + i, :GW] = packed
            parts_ref[q * held + i, GW : 2 * GW] = off
            parts_ref[q * held + i, 2 * GW :] = extra
            return 0

        lax.fori_loop(0, held, one, 0)

    def arrived(dst, sem):
        pltpu.make_async_remote_copy(
            src_ref=dst, dst_ref=dst, send_sem=send.at[0], recv_sem=sem,
            device_id=partner, device_id_type=pl.DeviceIdType.MESH,
        ).wait_recv()

    def to_partner(q):
        for i in range(held):
            n = q // 2 * held + i
            copy(parts_ref.at[q * held + i], swap.at[n], swap_recv.at[n], partner)

    compute(0)
    pl.semaphore_wait(barrier, 3 + jnp.minimum(z, 1) + jnp.minimum(zdim - 1 - z, 1))
    to_partner(0)
    compute(1)
    for i in range(held):
        arrived(swap.at[i], swap_recv.at[i])
        total[i] = parts_ref[held + i] + swap[i]
        copy(total.at[i], cross.at[i], cross_recv.at[i], beside)
    compute(2)
    to_partner(2)
    compute(3)
    base = bins * held + chan * nbins * held
    for i in range(held):
        arrived(swap.at[held + i], swap_recv.at[held + i])
        arrived(cross.at[i], cross_recv.at[i])
        out_ref[base + i] = (parts_ref[3 * held + i] + swap[held + i]) + cross[i]

    events = []
    for color, (_, _, order) in enumerate(COLORS):
        for dz in range(1 - zdim, zdim):
            for fx in range(2):
                for fy in range(2):
                    events.append((abs(dz) + fx + fy, fx + fy, color, dz, fx, fy))
    events.sort()
    for _, _, color, dz, fx, fy in events:
        first, count, order = COLORS[color]
        sz, sx, sy = z + dz, (1 - x if fx else x), (1 - y if fy else y)
        chip = (sz * ydim + sy) * 2 + sx
        there = None if dz == 0 else (z >= -dz if dz < 0 else z < zdim - dz)
        at = ((sz * ydim + sy) * nbins + sx * 2 + core) * held
        piece = out_ref.at[pl.ds(at, held), pl.ds(first, count)]
        offset = {"z": dz, "x": fx, "y": fy}
        last = max([n for n, d in enumerate(order) if offset[d]], default=-1)
        sem = recv.at[color, chip]
        if last >= 0:
            run(there, lambda piece=piece, sem=sem: arrived(piece, sem))

        def both(a, b):
            return b if a is None else (a if b is None else jnp.logical_and(a, b))

        if zdim > 1:
            onward = order.index("z") > last
            if (onward or (last >= 0 and order[last] == "z" and dz < 0)) and dz >= 2 - zdim:
                copy(piece, piece, sem, device(z + 1, y, x, core), both(there, above_there))
            if (onward or (last >= 0 and order[last] == "z" and dz > 0)) and dz <= zdim - 2:
                copy(piece, piece, sem, device(z - 1, y, x, core), both(there, below_there))
        if order.index("x") > last:
            copy(piece, piece, sem, beside, there)
        if order.index("y") > last:
            copy(piece, piece, sem, device(z, 1 - y, x, core), there)
        copy(piece, piece, drecv.at[color, chip], partner, there)

    for color, (first, count, _) in enumerate(COLORS):
        for chip in range(zdim * ydim * 2):
            at = (chip // 2 * nbins + chip % 2 * 2 + 1 - core) * held
            arrived(out_ref.at[pl.ds(at, held), pl.ds(first, count)], drecv.at[color, chip])
    for made, cond in issued:
        run(cond, made.wait_send)


def exchange(effects, nominal, observed, variance, theta, groups, counts):
    nbins, nchan = lax.axis_size("bins"), lax.axis_size("chan")
    chans, size, channel_width = effects.shape
    rows, width = 2 * GW + EXTRA, GW
    held = chans // nbins
    vmem = pl.BlockSpec(memory_space=pltpu.VMEM)
    smem = pl.BlockSpec(memory_space=pltpu.SMEM)
    chips = nchan * nbins // 2
    return pl.pallas_call(
        functools.partial(exchange_kernel, 2),
        in_specs=[smem, smem, pl.BlockSpec(memory_space=pltpu.HBM), vmem, vmem, vmem, vmem],
        out_specs=vmem,
        out_shape=jax.ShapeDtypeStruct((nchan * chans, rows, width), jnp.float32),
        scratch_shapes=[
            pltpu.VMEM((chans, size, channel_width), jnp.bfloat16),
            pltpu.VMEM((chans, rows, width), jnp.float32),
            pltpu.VMEM((2 * held, rows, width), jnp.float32),
            pltpu.VMEM((held, rows, width), jnp.float32),
            pltpu.VMEM((held, rows, width), jnp.float32),
            pltpu.SemaphoreType.DMA((chans,)),
            pltpu.SemaphoreType.DMA((2 * held,)),
            pltpu.SemaphoreType.DMA((held,)),
            pltpu.SemaphoreType.DMA((len(COLORS), chips)),
            pltpu.SemaphoreType.DMA((len(COLORS), chips)),
            pltpu.SemaphoreType.DMA((SENDS,)),
        ],
        compiler_params=pltpu.CompilerParams(
            collective_id=0, has_side_effects=True, vmem_limit_bytes=32 * 2**20
        ),
        name="exchange",
    )(groups, counts, pltpu.with_memory_space_constraint(effects, pltpu.HBM), nominal, observed, variance, theta.reshape(-1, 1, GW))


SENDS = 240


def local(effects, nominal, observed, mc_variance, theta, nuisance_index, bin_counts, tile_owner):
    devices = lax.axis_size("chan") * lax.axis_size("bins")
    device = lax.axis_index("chan") * lax.axis_size("bins") + lax.axis_index("bins")
    total_nu = theta.shape[0]
    slice_len = total_nu // devices
    groups = nuisance_index[:, ::GW] // GW
    arrays = (effects, nominal, observed, mc_variance, theta, groups, bin_counts)
    chan_size, bins_size = lax.axis_size("chan"), lax.axis_size("bins")
    if bins_size == 4 and chan_size % 2 == 0 and chan_size // 2 <= DEEP:
        payload = exchange(*arrays)
    else:
        summed = lax.psum_scatter(curvature(*arrays), "bins", scatter_dimension=0, tiled=True)
        payload = lax.all_gather(summed, ("chan", "bins"), axis=0, tiled=True)
    tiles, grad = place(
        payload, theta, groups, tile_owner, tile_owner.shape[0] // devices, max(1, slice_len // GW)
    )
    gradient = grad.reshape(-1)
    if slice_len < GW:
        gradient = lax.dynamic_slice_in_dim(gradient, device * slice_len % GW, slice_len, 0)
    return (tiles, gradient)


def solution(mesh):
    return jax.shard_map(
        local,
        mesh=mesh,
        in_specs=(
            P("chan", "bins", None),
            P("chan", "bins"),
            P("chan", "bins"),
            P("chan", "bins"),
            P(),
            P(),
            P("chan"),
            P(),
        ),
        out_specs=(P(("chan", "bins"), None, None), P(("chan", "bins"))),
        check_vma=False,
    )
```

profile of v0, /device:TPU:1, one launch (start us, length us, event | category | flops | bytes accessed | tf_op | source)
XLA Modules:
  0.0 72.2 jit_solution(2335474623953375753)
XLA Ops:
  0.6 0.9 %slice.3 = s32[64,2]{1,0:T(8,128)S(1)} slice(s32[64,256]{1,0:T(8,128)} %param.13), slice={[0:64:1], [0:256:128]} | slice | bytes 1024 | tf_op jit(solution)/shard_map/slice | solution.py:440
  1.6 0.0 copy-start
  1.6 0.7 %copy-done = f32[8192]{0:T(1024)S(1)} copy-done((f32[8192]{0:T(1024)S(1)}, f32[8192]{0:T(1024)}, u32[]{:S(2)}) %copy-start) | copy-done | bytes 32792
  2.3 0.0 copy-start.1
  2.3 0.8 %copy-done.1 = f32[8,2048]{1,0:T(8,128)S(1)} copy-done((f32[8,2048]{1,0:T(8,128)S(1)}, f32[8,2048]{1,0:T(8,128)}, u32[]{:S(2)}) %copy-start.1) | copy-done | bytes 65560
  3.2 0.0 copy-start.2
  3.2 0.8 %copy-done.2 = s32[8,2048]{1,0:T(8,128)S(1)} copy-done((s32[8,2048]{1,0:T(8,128)S(1)}, s32[8,2048]{1,0:T(8,128)}, u32[]{:S(2)}) %copy-start.2) | copy-done | bytes 65560
  4.0 0.0 copy-start.3
  4.0 0.8 %copy-done.3 = f32[8,2048]{1,0:T(8,128)S(1)} copy-done((f32[8,2048]{1,0:T(8,128)S(1)}, f32[8,2048]{1,0:T(8,128)}, u32[]{:S(2)}) %copy-start.3) | copy-done | bytes 65560
  4.9 0.0 copy-start.5
  4.9 0.7 copy-done.5
  5.5 0.0 copy-start.4
  5.5 57.5 %exchange.1.payload_ref = f32[64,264,128]{2,1,0:T(8,128)S(1)} custom-call(s32[64,2]{1,0:T(8,128)S(1)} %add_select_fusion.groups_ref, s32[8]{0:T(128)S(1)} %copy-done.5, bf16[8,2048,256]{2,1,0:T(8,128)(2,1)} %eff_ref.1, f32[8,2048]{1,0:T(8,128)S(1)} %copy-done.1, s32[8,2048]{1,0:T(8,128)S(1)} %copy-done.2, f32[8,2048]{1,0:T(8,128)S(1)} %copy-done.3, ...), custom_call_target="tpu_custom_call" | custom-call | tf_op jit(solution)/shard_map/exchange/pallas_call | solution.py:407
  63.0 0.0 copy-done.4
  63.0 9.2 %place.1 = (f32[8,512,512]{2,1,0:T(8,128)}, f32[2,1,128]{2,1,0:T(1,128)}) custom-call(s32[64,2]{1,0:T(8,128)S(1)} %add_select_fusion.groups_ref, s32[256]{0:T(256)S(1)} %copy-done.4, f32[64,264,128]{2,1,0:T(8,128)S(1)} %exchange.1.payload_ref, f32[64,1,128]{2,1,0:T(1,128)S(1)} %bitcast.3), custom_call_target="tpu_custom_call" | custom-call | tf_op jit(solution)/shard_map/place/pallas_call | solution.py:207
  (1 shorter events, 0.0 us)
Async XLA Ops:
  1.6 0.8 %copy-start = (f32[8192]{0:T(1024)S(1)}, f32[8192]{0:T(1024)}, u32[]{:S(2)}) copy-start(f32[8192]{0:T(1024)} %param.12) | copy-start | bytes 98308
  2.3 0.8 %copy-start.1 = (f32[8,2048]{1,0:T(8,128)S(1)}, f32[8,2048]{1,0:T(8,128)}, u32[]{:S(2)}) copy-start(f32[8,2048]{1,0:T(8,128)} %nom_ref.1) | copy-start | bytes 196612
  3.2 0.8 %copy-start.2 = (s32[8,2048]{1,0:T(8,128)S(1)}, s32[8,2048]{1,0:T(8,128)}, u32[]{:S(2)}) copy-start(s32[8,2048]{1,0:T(8,128)} %obs_ref.1) | copy-start | bytes 196612
  4.0 0.8 %copy-start.3 = (f32[8,2048]{1,0:T(8,128)S(1)}, f32[8,2048]{1,0:T(8,128)}, u32[]{:S(2)}) copy-start(f32[8,2048]{1,0:T(8,128)} %var_ref.1) | copy-start | bytes 196612
  4.9 0.7 copy-start.5
  5.5 57.5 %copy-start.4 = (s32[256]{0:T(256)S(1)}, s32[256]{0:T(256)}, u32[]{:S(2)}) copy-start(s32[256]{0:T(256)} %owner_ref.1) | copy-start | bytes 3076
where the time goes:
time: 73.4 us; the launch traced here: 72.2 us
  Pallas kernels  66.7 us (91%)
  local copies, waits for them, and re-layouts  4.85 us (7%)
    pallas_call x1, Pallas kernels, exchange(): pl.pallas_call(functools.partial(exchange_kernel, 2), in_specs=[smem, sme...  57.5 us
    pallas_call x1, Pallas kernels, place(): pl.pallas_call(place_kernel, grid_spec=pltpu.PrefetchScalarGridSpec(num_s...  9.17 us
    unnamed x12, local copies, waits for them, and re-layouts  3.93 us

commit v1 on v0

--- a/solution.py
+++ b/solution.py
@@ -234,42 +234,155 @@
     )(groups, tile_owner, payload, theta.reshape(-1, 1, GW))
 
 
-COLORS = ((0, 104, "zxy"), (104, 104, "zyx"), (208, 56, "xyz"))
+COLORS = ((0, 104, "zxy"), (104, 96, "zyx"), (200, 64, "xyz"))
 DEEP = 4
+LINKS = 5
+
+
+def exponent_rows(eff, chosen, nominal, observed, variance, live, left_ref):
+    eff_t = eff.T
+    exponent = jnp.dot(chosen, eff_t, preferred_element_type=jnp.float32)[0:8]
+    expected = nominal * jnp.exp(exponent)
+    denominator = 1.0 + expected * variance
+    residual = jnp.where(live, (expected - observed) / denominator, 0.0)
+    weight = jnp.where(live, expected / denominator, 0.0)
+    left_ref[: 2 * GW] = (eff_t.astype(jnp.float32) * weight[0:1]).astype(jnp.bfloat16)
+    left_ref[2 * GW :] = jnp.concatenate([residual, residual], axis=0).astype(jnp.bfloat16)
+
+
+def block_rows(left, eff):
+    full = jnp.dot(left, eff, preferred_element_type=jnp.float32)
+    first, off, second = full[:GW, :GW], full[:GW, GW:], full[GW : 2 * GW, GW:]
+    row = lax.broadcasted_iota(jnp.int32, (GW, GW), 0)
+    col = lax.broadcasted_iota(jnp.int32, (GW, GW), 1)
+    packed = jnp.where(row <= col, first, second)
+    second_diag = jnp.sum(jnp.where(row == col, second, 0.0), axis=0, keepdims=True)
+    grad0 = full[2 * GW : 2 * GW + 8, :GW]
+    grad1 = full[2 * GW : 2 * GW + 8, GW:]
+    which = lax.broadcasted_iota(jnp.int32, (EXTRA, GW), 0)
+    extra = jnp.where(
+        which == 0, grad0, jnp.where(which == 1, grad1, jnp.broadcast_to(second_diag, (EXTRA, GW)))
+    )
+    return packed, off, extra
+
+
+def make_plan(index_ref, mine, total_groups, plan_ref):
+    per_tile = TILE // GW
+    shift = per_tile.bit_length() - 1
+    side = total_groups // per_tile
+    chans = index_ref.shape[0]
+    slots = len(mine)
+    count = 4 * chans
+    gshift = GW.bit_length() - 1
+    a, b = index_ref[:, :GW] >> gshift, index_ref[:, GW:] >> gshift
+    ta, tb = a >> shift, b >> shift
+    ra, rb = a & (per_tile - 1), b & (per_tile - 1)
+    c = lax.broadcasted_iota(jnp.int32, (chans, GW), 0)
+    keys, codes, places = [], [], []
+    cases = ((ta, ta, ra, ra), (tb, tb, rb, rb), (ta, tb, ra, rb), (tb, ta, rb, ra))
+    for kind, (tr, tc, rr, rc) in enumerate(cases):
+        tile = tr * side + tc
+        slot = jnp.full((chans, GW), slots, jnp.int32)
+        for s in range(slots):
+            slot = jnp.where(tile == mine[s], s, slot)
+        places.append(slot)
+        keys.append(slot * count + kind * chans + c)
+        codes.append(((((c << shift) + rr) << shift) + rc) * 4 + kind)
+    key = jnp.concatenate(keys, axis=0)
+    code = jnp.concatenate(codes, axis=0).astype(jnp.float32)
+    place_col = jnp.concatenate(places, axis=0)
+    lane = lax.broadcasted_iota(jnp.int32, (count, GW), 1)
+    key_rows = key.T
+    rank = jnp.zeros((count, 1), jnp.float32)
+    for j in range(0, count, GW):
+        less = jnp.where(key_rows[0:1, j : j + GW] < key, 1.0, 0.0)
+        rank += jnp.sum(less, axis=1, keepdims=True)
+    rank = jnp.broadcast_to(rank, (count, GW)).astype(jnp.int32)
+    for j in range(0, count, GW):
+        picked = jnp.sum(jnp.where(rank == lane + j, code, 0.0), axis=0, keepdims=True)
+        plan_ref[0:1, j : j + GW] = picked.astype(jnp.int32)
+    starts = jnp.sum(jnp.where(place_col < lane, 1.0, 0.0), axis=0, keepdims=True)
+    plan_ref[1:2, 0:GW] = starts.astype(jnp.int32)
+    lane1 = lax.broadcasted_iota(jnp.int32, (1, GW), 1)
+    diagonal = jnp.zeros((1, GW), jnp.int32)
+    for s in range(slots):
+        t = jnp.full((1, GW), mine[s], jnp.int32)
+        on = (t >> (side.bit_length() - 1)) == (t & (side - 1))
+        diagonal = jnp.where(jnp.logical_and(lane1 == s, on), 1, diagonal)
+    plan_ref[2:3, 0:GW] = diagonal
 
 
 def exchange_kernel(
-    ydim, groups_ref, counts_ref, eff_ref, nom_ref, obs_ref, var_ref, theta_ref, out_ref,
-    eff_held, parts_ref, swap, cross, total, eff_sem, swap_recv, cross_recv, recv, drecv, send,
+    ydim, slots, index_hbm, counts_hbm, eff_hbm, nom_hbm, obs_hbm, var_hbm, theta_hbm, owner_hbm,
+    out_ref, plan_ref,
+    eff_held, parts_ref, swap, cross, total, left, nom_ref, obs_ref, var_ref, theta_ref, index_ref,
+    local_index, counts_ref, owner_ref,
+    eff_sem, small_sem, swap_recv, cross_recv, recv, drecv, send,
 ):
     chan, bins = lax.axis_index("chan"), lax.axis_index("bins")
     zdim = lax.axis_size("chan") // ydim
     nbins = lax.axis_size("bins")
     z, y = chan // ydim, chan % ydim
     x, core = bins // 2, bins % 2
-    held = parts_ref.shape[0] // nbins
-    issued = []
+    chans, size = eff_held.shape[:2]
+    held = chans // nbins
+    sent = {}
+    colors = len(COLORS)
 
     def device(zz, yy, xx, kk):
         return {"chan": zz * ydim + yy, "bins": xx * 2 + kk}
-
-    def copy(src, dst, recv_sem, target, cond=None):
-        made = pltpu.make_async_remote_copy(
-            src_ref=src,
-            dst_ref=dst,
-            send_sem=send.at[len(issued)],
-            recv_sem=recv_sem,
-            device_id=target,
-            device_id_type=pl.DeviceIdType.MESH,
-        )
-        issued.append((made, cond))
-        run(cond, made.start)
 
     def run(cond, action):
         if cond is None:
             action()
         else:
             pl.when(cond)(action)
+
+    def copy(src, dst, recv_sem, target, group, there=None):
+        made = pltpu.make_async_remote_copy(
+            src_ref=src,
+            dst_ref=dst,
+            send_sem=send.at[group],
+            recv_sem=recv_sem,
+            device_id=target,
+            device_id_type=pl.DeviceIdType.MESH,
+        )
+        cond, places = (None, range(zdim)) if there is None else there
+        counted = sent.setdefault(group, [0] * zdim)
+        for place in places:
+            counted[place] += 1
+        run(cond, made.start)
+
+    far, near = (1 - x) * 2, x * 2
+    owners = (far + 1 - core, far + core, near + 1 - core, near + core)
+
+    def load(q, h):
+        at = q * held + h
+        return pltpu.make_async_copy(eff_hbm.at[owners[q] * held + h], eff_held.at[at], eff_sem.at[at])
+
+    mine_rows = pl.ds(pl.multiple_of(chan * chans, chans), chans)
+    smalls = [
+        (index_hbm.at[mine_rows], local_index),
+        (counts_hbm, counts_ref),
+        (theta_hbm, theta_ref),
+        (nom_hbm, nom_ref),
+        (var_hbm, var_ref),
+        (obs_hbm, obs_ref),
+        (owner_hbm, owner_ref),
+        (index_hbm, index_ref),
+    ]
+    smalls = [pltpu.make_async_copy(a, b, small_sem.at[n]) for n, (a, b) in enumerate(smalls)]
+    for made in smalls[:3]:
+        made.start()
+    load(0, 0).start()
+    for made in smalls[3:6]:
+        made.start()
+    for h in range(held):
+        for q in range(4):
+            if (q, h) != (0, 0):
+                load(q, h).start()
+    for made in smalls[6:]:
+        made.start()
 
     partner = device(z, y, x, 1 - core)
     beside = device(z, y, 1 - x, core)
@@ -286,44 +399,44 @@
         run(cond, lambda target=target: pl.semaphore_signal(
             barrier, 1, device_id=target, device_id_type=pl.DeviceIdType.MESH
         ))
-    far, near = (1 - x) * 2, x * 2
-    owners = (far + 1 - core, far + core, near + 1 - core, near + core)
-    size = eff_ref.shape[1]
-
-    def load(q, i):
-        at = q * held + i
-        return pltpu.make_async_copy(eff_ref.at[owners[q] * held + i], eff_held.at[at], eff_sem.at[at])
-
-    for q in range(4):
-        for i in range(held):
-            load(q, i).start()
-
-    def compute(q):
-        for i in range(held):
-            load(q, i).wait()
-
-        def one(i, _):
-            c = owners[q] * held + i
-            base = chan * nbins * held + c
-            g0, g1 = groups_ref[base, 0], groups_ref[base, 1]
-            chosen = jnp.concatenate([theta_ref[g0], theta_ref[g1]], axis=1).astype(jnp.bfloat16)
-            chosen = jnp.broadcast_to(chosen, (16, 2 * GW))
-            line = pl.ds(c, 1)
-            position = bins * size + lax.broadcasted_iota(jnp.int32, (8, size), 1)
-            packed, off, extra = channel_payload(
-                eff_held[q * held + i],
-                chosen,
-                nom_ref[line],
-                obs_ref[line].astype(jnp.float32),
-                var_ref[line],
-                position < counts_ref[c],
-            )
-            parts_ref[q * held + i, :GW] = packed
-            parts_ref[q * held + i, GW : 2 * GW] = off
-            parts_ref[q * held + i, 2 * GW :] = extra
-            return 0
-
-        lax.fori_loop(0, held, one, 0)
+    for made in smalls[:6]:
+        made.wait()
+
+    def prepare(q, h):
+        c = owners[q] * held + h
+        g0 = local_index[c, 0] >> (GW.bit_length() - 1)
+        g1 = local_index[c, GW] >> (GW.bit_length() - 1)
+        chosen = jnp.concatenate([theta_ref[g0], theta_ref[g1]], axis=1).astype(jnp.bfloat16)
+        chosen = jnp.broadcast_to(chosen, (16, 2 * GW))
+        line = pl.ds(c, 1)
+        position = bins * size + lax.broadcasted_iota(jnp.int32, (8, size), 1)
+        exponent_rows(
+            eff_held[q * held + h],
+            chosen,
+            nom_ref[line],
+            obs_ref[line].astype(jnp.float32),
+            var_ref[line],
+            position < counts_ref[c],
+            left.at[q % 2],
+        )
+
+    def multiply(q, h):
+        packed, off, extra = block_rows(left[q % 2], eff_held[q * held + h])
+        at = q * held + h
+        parts_ref[at, :GW] = packed
+        parts_ref[at, GW : 2 * GW] = off
+        parts_ref[at, 2 * GW :] = extra
+
+    steps = [(q, h) for h in range(held) for q in range(4)]
+
+    def compute(n):
+        if n == 0:
+            load(*steps[0]).wait()
+            prepare(*steps[0])
+        if n + 1 < len(steps):
+            load(*steps[n + 1]).wait()
+            prepare(*steps[n + 1])
+        multiply(*steps[n])
 
     def arrived(dst, sem):
         pltpu.make_async_remote_copy(
@@ -331,105 +444,304 @@
             device_id=partner, device_id_type=pl.DeviceIdType.MESH,
         ).wait_recv()
 
-    def to_partner(q):
-        for i in range(held):
-            n = q // 2 * held + i
-            copy(parts_ref.at[q * held + i], swap.at[n], swap_recv.at[n], partner)
-
-    compute(0)
-    pl.semaphore_wait(barrier, 3 + jnp.minimum(z, 1) + jnp.minimum(zdim - 1 - z, 1))
-    to_partner(0)
-    compute(1)
-    for i in range(held):
-        arrived(swap.at[i], swap_recv.at[i])
-        total[i] = parts_ref[held + i] + swap[i]
-        copy(total.at[i], cross.at[i], cross_recv.at[i], beside)
-    compute(2)
-    to_partner(2)
-    compute(3)
-    base = bins * held + chan * nbins * held
-    for i in range(held):
-        arrived(swap.at[held + i], swap_recv.at[held + i])
-        arrived(cross.at[i], cross_recv.at[i])
-        out_ref[base + i] = (parts_ref[3 * held + i] + swap[held + i]) + cross[i]
-
-    events = []
-    for color, (_, _, order) in enumerate(COLORS):
-        for dz in range(1 - zdim, zdim):
-            for fx in range(2):
-                for fy in range(2):
-                    events.append((abs(dz) + fx + fy, fx + fy, color, dz, fx, fy))
-    events.sort()
-    for _, _, color, dz, fx, fy in events:
+    def to_partner(q, h):
+        n = q // 2 * held + h
+        copy(parts_ref.at[q * held + h], swap.at[n], swap_recv.at[n], partner, LINKS * colors)
+
+    def send_across(h):
+        arrived(swap.at[h], swap_recv.at[h])
+        total[h] = parts_ref[held + h] + swap[h]
+        for color, (first, count, _) in enumerate(COLORS):
+            rows = pl.ds(first, count)
+            copy(total.at[h, rows], cross.at[h, rows], cross_recv.at[h, color], beside, 2 * colors + color)
+
+    own = (chan * nbins + bins) * held
+
+    def finish(h, color):
+        first, count, _ = COLORS[color]
+        rows = pl.ds(first, count)
+        arrived(cross.at[h, rows], cross_recv.at[h, color])
+        out_ref[own + h, rows] = (
+            parts_ref[3 * held + h, rows] + swap[held + h, rows]
+        ) + cross[h, rows]
+
+    def forward(h, color, dz, fx, fy):
         first, count, order = COLORS[color]
         sz, sx, sy = z + dz, (1 - x if fx else x), (1 - y if fy else y)
         chip = (sz * ydim + sy) * 2 + sx
         there = None if dz == 0 else (z >= -dz if dz < 0 else z < zdim - dz)
-        at = ((sz * ydim + sy) * nbins + sx * 2 + core) * held
-        piece = out_ref.at[pl.ds(at, held), pl.ds(first, count)]
+        places = [p for p in range(zdim) if 0 <= p + dz < zdim]
+        at = ((sz * ydim + sy) * nbins + sx * 2 + core) * held + h
+        piece = out_ref.at[at, pl.ds(first, count)]
         offset = {"z": dz, "x": fx, "y": fy}
         last = max([n for n, d in enumerate(order) if offset[d]], default=-1)
-        sem = recv.at[color, chip]
+        sem = recv.at[h, color, chip]
         if last >= 0:
-            run(there, lambda piece=piece, sem=sem: arrived(piece, sem))
+            run(there, lambda: arrived(piece, sem))
 
         def both(a, b):
             return b if a is None else (a if b is None else jnp.logical_and(a, b))
 
+        here = (there, places)
         if zdim > 1:
             onward = order.index("z") > last
             if (onward or (last >= 0 and order[last] == "z" and dz < 0)) and dz >= 2 - zdim:
-                copy(piece, piece, sem, device(z + 1, y, x, core), both(there, above_there))
+                up = (both(there, above_there), [p for p in places if p < zdim - 1])
+                copy(piece, piece, sem, device(z + 1, y, x, core), color, up)
             if (onward or (last >= 0 and order[last] == "z" and dz > 0)) and dz <= zdim - 2:
-                copy(piece, piece, sem, device(z - 1, y, x, core), both(there, below_there))
+                down = (both(there, below_there), [p for p in places if p > 0])
+                copy(piece, piece, sem, device(z - 1, y, x, core), colors + color, down)
         if order.index("x") > last:
-            copy(piece, piece, sem, beside, there)
+            copy(piece, piece, sem, beside, 2 * colors + color, here)
         if order.index("y") > last:
-            copy(piece, piece, sem, device(z, 1 - y, x, core), there)
-        copy(piece, piece, drecv.at[color, chip], partner, there)
-
-    for color, (first, count, _) in enumerate(COLORS):
-        for chip in range(zdim * ydim * 2):
-            at = (chip // 2 * nbins + chip % 2 * 2 + 1 - core) * held
-            arrived(out_ref.at[pl.ds(at, held), pl.ds(first, count)], drecv.at[color, chip])
-    for made, cond in issued:
-        run(cond, made.wait_send)
-
-
-def exchange(effects, nominal, observed, variance, theta, groups, counts):
+            copy(piece, piece, sem, device(z, 1 - y, x, core), 3 * colors + color, here)
+        copy(piece, piece, drecv.at[color], partner, 4 * colors + color, here)
+
+    compute(0)
+    pl.semaphore_wait(barrier, 3 + jnp.minimum(z, 1) + jnp.minimum(zdim - 1 - z, 1))
+    to_partner(0, 0)
+    compute(1)
+    send_across(0)
+    compute(2)
+    to_partner(2, 0)
+    compute(3)
+    compute(4)
+    to_partner(0, 1)
+    compute(5)
+    send_across(1)
+    arrived(swap.at[held], swap_recv.at[held])
+    finish(0, 0)
+    forward(0, 0, 0, 0, 0)
+    compute(6)
+    to_partner(2, 1)
+    finish(0, 1)
+    forward(0, 1, 0, 0, 0)
+    compute(7)
+    finish(0, 2)
+    forward(0, 2, 0, 0, 0)
+    arrived(swap.at[held + 1], swap_recv.at[held + 1])
+    order = [e for e in ORDER if abs(e[2]) < zdim]
+    for n, e in enumerate(order):
+        if n == PLAN_AT:
+            for made in smalls[6:]:
+                made.wait()
+            me = (chan * nbins + bins) * slots
+            make_plan(
+                index_ref, [owner_ref[me + s] for s in range(slots)], theta_ref.shape[0], plan_ref
+            )
+        h, color, dz, fx, fy = e
+        if (dz, fx, fy) == (0, 0, 0):
+            finish(h, color)
+        forward(*e)
+
+    chips = zdim * ydim * 2
+
+    def waiting(n, count, group, color):
+        part = out_ref.at[pl.ds(0, n), pl.ds(0, count)]
+        return pltpu.make_async_remote_copy(
+            src_ref=part, dst_ref=part, send_sem=send.at[group], recv_sem=drecv.at[color],
+            device_id=partner, device_id_type=pl.DeviceIdType.MESH,
+        )
+
+    for color, (_, count, _) in enumerate(COLORS):
+        waiting(held * chips, count, 0, color).wait_recv()
+    for group, numbers in sent.items():
+        count = COLORS[group % colors][1] if group < LINKS * colors else out_ref.shape[1]
+        if len(set(numbers)) == 1:
+            waiting(numbers[0], count, group, 0).wait_send()
+            continue
+        for place, number in enumerate(numbers):
+            if number:
+                pl.when(z == place)(waiting(number, count, group, 0).wait_send)
+
+
+ORDER = (
+    (1, 0, 0, 0, 0), (1, 1, 0, 0, 0), (1, 2, 0, 0, 0), (0, 0, -1, 0, 0), (0, 0, 1, 0, 0),
+    (0, 1, -1, 0, 0), (1, 0, 1, 0, 0), (0, 1, 0, 0, 1), (1, 1, 1, 0, 0), (1, 0, -1, 0, 0),
+    (1, 1, -1, 0, 0), (0, 2, -1, 0, 0), (0, 2, 0, 1, 0), (0, 0, 2, 0, 0), (0, 0, 0, 0, 1),
+    (0, 0, 0, 1, 0), (1, 2, 0, 1, 0), (1, 0, -2, 0, 0), (0, 1, 1, 0, 0), (1, 2, 0, 0, 1),
+    (0, 0, 1, 0, 1), (1, 0, 2, 0, 0), (0, 0, -2, 0, 0), (0, 2, 0, 0, 1), (1, 2, -1, 1, 0),
+    (1, 0, 0, 1, 0), (0, 2, 1, 1, 0), (1, 1, 2, 0, 0), (1, 1, -2, 0, 0), (0, 2, 0, 1, 1),
+    (1, 0, -3, 0, 0), (0, 1, -2, 0, 0), (0, 1, 2, 0, 0), (0, 2, 1, 0, 0), (0, 1, -1, 0, 1),
+    (0, 0, -3, 0, 0), (1, 0, 3, 0, 0), (1, 0, 1, 0, 1), (1, 1, -3, 0, 0), (1, 0, -3, 1, 0),
+    (0, 2, -1, 1, 0), (0, 2, -1, 0, 1), (0, 2, 2, 1, 0), (1, 0, -1, 1, 0), (1, 2, 1, 0, 0),
+    (1, 1, 1, 0, 1), (1, 1, 3, 0, 0), (1, 2, -1, 0, 0), (0, 0, 2, 1, 0), (0, 1, 3, 0, 0),
+    (1, 1, 0, 0, 1), (1, 2, 0, 1, 1), (1, 0, -2, 1, 0), (0, 1, -3, 0, 0), (1, 2, 1, 0, 1),
+    (0, 0, 3, 0, 0), (1, 2, 1, 1, 0), (1, 1, 3, 1, 0), (0, 2, 1, 0, 1), (0, 0, -2, 0, 1),
+    (1, 2, -1, 0, 1), (1, 2, -2, 1, 0), (1, 1, -3, 0, 1), (1, 0, -1, 0, 1), (0, 2, 3, 1, 0),
+    (1, 0, 1, 1, 0), (0, 2, 2, 0, 0), (1, 0, -2, 0, 1), (1, 0, -3, 0, 1), (0, 1, 1, 0, 1),
+    (0, 2, -2, 0, 0), (0, 2, -1, 1, 1), (1, 0, 3, 1, 0), (0, 2, 1, 1, 1), (1, 1, -3, 1, 0),
+    (1, 1, 3, 0, 1), (0, 2, -2, 0, 1), (1, 0, 2, 1, 0), (1, 1, -2, 0, 1), (1, 0, 0, 1, 1),
+    (0, 1, -2, 0, 1), (1, 0, 3, 0, 1), (1, 2, -1, 1, 1), (0, 0, -2, 1, 0), (0, 1, 1, 1, 0),
+    (1, 1, 0, 1, 0), (0, 1, 3, 0, 1), (0, 0, -3, 1, 0), (1, 2, -2, 0, 0), (1, 2, 2, 0, 0),
+    (0, 1, 2, 0, 1), (0, 0, -1, 0, 1), (0, 2, 3, 0, 0), (1, 2, 1, 1, 1), (1, 2, 2, 0, 1),
+    (0, 0, 3, 1, 0), (1, 2, -2, 0, 1), (0, 1, -3, 1, 0), (0, 1, 2, 1, 0), (1, 1, 2, 0, 1),
+    (1, 1, -1, 0, 1), (0, 0, 1, 1, 0), (1, 1, -3, 1, 1), (0, 2, -2, 1, 0), (0, 2, 2, 0, 1),
+    (0, 0, 2, 0, 1), (0, 2, -2, 1, 1), (1, 1, 1, 1, 0), (1, 0, 2, 0, 1), (0, 1, 3, 1, 0),
+    (0, 1, 3, 1, 1), (0, 0, -1, 1, 0), (0, 1, -3, 0, 1), (1, 2, 2, 1, 0), (0, 0, -3, 1, 1),
+    (1, 2, -3, 1, 0), (0, 2, -3, 1, 0), (0, 1, 0, 1, 0), (0, 2, 3, 1, 1), (1, 2, 3, 0, 0),
+    (1, 2, -2, 1, 1), (0, 2, -3, 0, 0), (0, 0, -2, 1, 1), (0, 0, -3, 0, 1), (0, 1, 0, 1, 1),
+    (0, 0, 3, 1, 1), (0, 0, 3, 0, 1), (1, 0, 3, 1, 1), (1, 2, -3, 0, 0), (1, 0, -2, 1, 1),
+    (0, 0, 0, 1, 1), (0, 1, -1, 1, 0), (0, 1, -1, 1, 1), (1, 1, 0, 1, 1), (1, 0, -1, 1, 1),
+    (0, 1, -2, 1, 0), (1, 1, 1, 1, 1), (1, 2, 3, 0, 1), (0, 0, 2, 1, 1), (1, 0, 0, 0, 1),
+    (0, 2, 2, 1, 1), (0, 2, 3, 0, 1), (1, 2, 2, 1, 1), (1, 0, 1, 1, 1), (1, 1, -2, 1, 1),
+    (1, 1, 2, 1, 0), (0, 2, -3, 1, 1), (0, 0, 1, 1, 1), (0, 1, -2, 1, 1), (0, 1, 2, 1, 1),
+    (1, 0, -3, 1, 1), (1, 2, -3, 0, 1), (0, 2, -3, 0, 1), (0, 1, 1, 1, 1), (1, 1, -2, 1, 0),
+    (1, 1, -1, 1, 0), (1, 2, 3, 1, 0), (0, 0, -1, 1, 1), (1, 1, 2, 1, 1), (0, 1, -3, 1, 1),
+    (1, 0, 2, 1, 1), (1, 1, 3, 1, 1), (1, 2, 3, 1, 1), (1, 1, -1, 1, 1), (1, 2, -3, 1, 1),
+)
+PLAN_AT = 40
+
+
+def exchange(effects, nominal, observed, variance, theta, nuisance_index, counts, tile_owner):
     nbins, nchan = lax.axis_size("bins"), lax.axis_size("chan")
     chans, size, channel_width = effects.shape
     rows, width = 2 * GW + EXTRA, GW
     held = chans // nbins
+    hbm = pl.BlockSpec(memory_space=pltpu.HBM)
     vmem = pl.BlockSpec(memory_space=pltpu.VMEM)
-    smem = pl.BlockSpec(memory_space=pltpu.SMEM)
     chips = nchan * nbins // 2
+    slots = tile_owner.shape[0] // (nchan * nbins)
+    colors = len(COLORS)
+    operands = (
+        nuisance_index, counts, effects, nominal, observed, variance,
+        theta.reshape(-1, 1, GW), tile_owner,
+    )
     return pl.pallas_call(
-        functools.partial(exchange_kernel, 2),
-        in_specs=[smem, smem, pl.BlockSpec(memory_space=pltpu.HBM), vmem, vmem, vmem, vmem],
-        out_specs=vmem,
-        out_shape=jax.ShapeDtypeStruct((nchan * chans, rows, width), jnp.float32),
+        functools.partial(exchange_kernel, 2, slots),
+        in_specs=[hbm] * len(operands),
+        out_specs=[vmem, vmem],
+        out_shape=[
+            jax.ShapeDtypeStruct((nchan * chans, rows, width), jnp.float32),
+            jax.ShapeDtypeStruct((8, 4 * nchan * chans), jnp.int32),
+        ],
         scratch_shapes=[
             pltpu.VMEM((chans, size, channel_width), jnp.bfloat16),
             pltpu.VMEM((chans, rows, width), jnp.float32),
             pltpu.VMEM((2 * held, rows, width), jnp.float32),
             pltpu.VMEM((held, rows, width), jnp.float32),
             pltpu.VMEM((held, rows, width), jnp.float32),
+            pltpu.VMEM((2, channel_width + 16, size), jnp.bfloat16),
+            pltpu.VMEM(nominal.shape, nominal.dtype),
+            pltpu.VMEM(observed.shape, observed.dtype),
+            pltpu.VMEM(variance.shape, variance.dtype),
+            pltpu.VMEM((theta.shape[0] // GW, 1, GW), theta.dtype),
+            pltpu.VMEM(nuisance_index.shape, jnp.int32),
+            pltpu.SMEM((chans, nuisance_index.shape[1]), jnp.int32),
+            pltpu.SMEM(counts.shape, jnp.int32),
+            pltpu.SMEM(tile_owner.shape, jnp.int32),
             pltpu.SemaphoreType.DMA((chans,)),
+            pltpu.SemaphoreType.DMA((8,)),
             pltpu.SemaphoreType.DMA((2 * held,)),
-            pltpu.SemaphoreType.DMA((held,)),
-            pltpu.SemaphoreType.DMA((len(COLORS), chips)),
-            pltpu.SemaphoreType.DMA((len(COLORS), chips)),
-            pltpu.SemaphoreType.DMA((SENDS,)),
+            pltpu.SemaphoreType.DMA((held, colors)),
+            pltpu.SemaphoreType.DMA((held, colors, chips)),
+            pltpu.SemaphoreType.DMA((colors,)),
+            pltpu.SemaphoreType.DMA((LINKS * colors + 1,)),
         ],
         compiler_params=pltpu.CompilerParams(
             collective_id=0, has_side_effects=True, vmem_limit_bytes=32 * 2**20
         ),
         name="exchange",
-    )(groups, counts, pltpu.with_memory_space_constraint(effects, pltpu.HBM), nominal, observed, variance, theta.reshape(-1, 1, GW))
-
-
-SENDS = 240
+    )(*[pltpu.with_memory_space_constraint(a, pltpu.HBM) for a in operands])
+
+
+def fill_kernel(plan_ref, payload_ref, index_ref, theta_ref, tiles_ref, grad_ref, held_tiles, sems):
+    slots = held_tiles.shape[0]
+    per_tile = TILE // GW
+    shift = per_tile.bit_length() - 1
+    row = lax.broadcasted_iota(jnp.int32, (GW, GW), 0)
+    col = lax.broadcasted_iota(jnp.int32, (GW, GW), 1)
+    eye = (row == col).astype(jnp.float32)
+
+    def put(s):
+        return pltpu.make_async_copy(held_tiles.at[s], tiles_ref.at[s], sems.at[s])
+
+    def one_tile(s, _):
+        held_tiles[s] = jnp.zeros((TILE, TILE), jnp.float32)
+
+        @pl.when(plan_ref[2, s] == 1)
+        def _():
+            for r in range(per_tile):
+                held_tiles[s, r * GW : (r + 1) * GW, r * GW : (r + 1) * GW] = eye
+
+        def accumulate(i, _):
+            code = plan_ref[0, i]
+            kind = code & 3
+            rc = (code >> 2) & (per_tile - 1)
+            rr = (code >> (2 + shift)) & (per_tile - 1)
+            c = code >> (2 + 2 * shift)
+            at = (
+                s,
+                pl.ds(pl.multiple_of(rr * GW, GW), GW),
+                pl.ds(pl.multiple_of(rc * GW, GW), GW),
+            )
+
+            @pl.when(kind == 0)
+            def _():
+                block = payload_ref[c, :GW]
+                held_tiles[at] += jnp.where(row <= col, block, block.T)
+
+            @pl.when(kind == 1)
+            def _():
+                block = payload_ref[c, :GW]
+                diag = jnp.where(row == col, payload_ref[c, 2 * GW + 2 : 2 * GW + 3], block.T)
+                held_tiles[at] += jnp.where(row > col, block, diag)
+
+            @pl.when(kind == 2)
+            def _():
+                held_tiles[at] += payload_ref[c, GW : 2 * GW]
+
+            @pl.when(kind == 3)
+            def _():
+                held_tiles[at] += payload_ref[c, GW : 2 * GW].T
+
+            return 0
+
+        lax.fori_loop(plan_ref[1, s], plan_ref[1, s + 1], accumulate, 0)
+        put(s).start()
+        return 0
+
+    lax.fori_loop(0, slots, one_tile, 0)
+
+    mine = grad_ref.shape[0]
+    device = lax.axis_index("chan") * lax.axis_size("bins") + lax.axis_index("bins")
+    total_groups = theta_ref.shape[0]
+    first = device * total_groups // (lax.axis_size("chan") * lax.axis_size("bins"))
+    gshift = GW.bit_length() - 1
+    for m in range(mine):
+        acc = theta_ref[first + m]
+        for r in range(2):
+            hit = (index_ref[:, r * GW : (r + 1) * GW] >> gshift) == first + m
+            acc += jnp.sum(jnp.where(hit, payload_ref[:, 2 * GW + r], 0.0), axis=0, keepdims=True)
+        grad_ref[m] = acc
+
+    def drain(s, _):
+        put(s).wait()
+        return 0
+
+    lax.fori_loop(0, slots, drain, 0)
+
+
+def fill(payload, plan, theta, nuisance_index, slots, mine):
+    chans, rows = payload.shape[:2]
+    vmem = pl.BlockSpec(memory_space=pltpu.VMEM)
+    return pl.pallas_call(
+        fill_kernel,
+        in_specs=[pl.BlockSpec(memory_space=pltpu.SMEM), vmem, vmem, vmem],
+        out_specs=[pl.BlockSpec(memory_space=pltpu.HBM), vmem],
+        out_shape=[
+            jax.ShapeDtypeStruct((slots, TILE, TILE), jnp.float32),
+            jax.ShapeDtypeStruct((mine, 1, GW), jnp.float32),
+        ],
+        scratch_shapes=[
+            pltpu.VMEM((slots, TILE, TILE), jnp.float32),
+            pltpu.SemaphoreType.DMA((slots,)),
+        ],
+        compiler_params=pltpu.CompilerParams(
+            vmem_limit_bytes=4 * chans * (rows + EXTRA) * GW + 4 * slots * TILE * TILE + 4 * 2**20
+        ),
+        name="fill",
+    )(plan, payload, nuisance_index, theta.reshape(-1, 1, GW))
 
 
 def local(effects, nominal, observed, mc_variance, theta, nuisance_index, bin_counts, tile_owner):
@@ -437,17 +749,19 @@
     device = lax.axis_index("chan") * lax.axis_size("bins") + lax.axis_index("bins")
     total_nu = theta.shape[0]
     slice_len = total_nu // devices
-    groups = nuisance_index[:, ::GW] // GW
-    arrays = (effects, nominal, observed, mc_variance, theta, groups, bin_counts)
+    slots, mine = tile_owner.shape[0] // devices, max(1, slice_len // GW)
     chan_size, bins_size = lax.axis_size("chan"), lax.axis_size("bins")
-    if bins_size == 4 and chan_size % 2 == 0 and chan_size // 2 <= DEEP:
-        payload = exchange(*arrays)
+    if bins_size == 4 and chan_size % 2 == 0 and chan_size // 2 <= DEEP and effects.shape[0] == 2 * bins_size and slice_len >= GW:
+        payload, plan = exchange(
+            effects, nominal, observed, mc_variance, theta, nuisance_index, bin_counts, tile_owner
+        )
+        tiles, grad = fill(payload, plan, theta, nuisance_index, slots, mine)
     else:
+        groups = nuisance_index[:, ::GW] // GW
+        arrays = (effects, nominal, observed, mc_variance, theta, groups, bin_counts)
         summed = lax.psum_scatter(curvature(*arrays), "bins", scatter_dimension=0, tiled=True)
         payload = lax.all_gather(summed, ("chan", "bins"), axis=0, tiled=True)
-    tiles, grad = place(
-        payload, theta, groups, tile_owner, tile_owner.shape[0] // devices, max(1, slice_len // GW)
-    )
+        tiles, grad = place(payload, theta, groups, tile_owner, slots, mine)
     gradient = grad.reshape(-1)
     if slice_len < GW:
         gradient = lax.dynamic_slice_in_dim(gradient, device * slice_len % GW, slice_len, 0)

time: 73.4 us -> 54.3 us (0.74)
  Pallas kernels: 66.7 us -> 52.8 us
  local copies, waits for them, and re-layouts: 4.85 us -> 0.01 us
    pallas_call x2, Pallas kernels: 66.7 us -> 52.8 us  [the longest x1 48 us: exchange(): pl.pallas_call(functools.partial(exchange_kernel, 2, slots), in_specs=[hb...]
    unnamed x12 -> x4, local copies, waits for them, and re-layouts: 3.93 us -> 0.01 us
    slice x1 -> x0, local copies, waits for them, and re-layouts: 0.92 us -> none  [local(): groups = nuisance_index[:, ::GW] // GW]
where the time goes in v1:
time: 54.3 us; the launch traced here: 53.5 us
  Pallas kernels  52.8 us (97%)
  between operations  0.67 us (1%)
    pallas_call x1, Pallas kernels, exchange(): pl.pallas_call(functools.partial(exchange_kernel, 2, slots), in_specs=[hb...  48 us
    pallas_call x1, Pallas kernels, fill(): pl.pallas_call(fill_kernel, in_specs=[pl.BlockSpec(memory_space=pltpu.SME...  4.8 us

profile of v1, /device:TPU:1, one launch (start us, length us, event | category | flops | bytes accessed | tf_op | source)
XLA Modules:
  0.0 53.5 jit_solution(4630657593612669341)
XLA Ops:
  0.6 0.0 copy-start
  0.6 0.0 copy-start.1
  0.7 48.0 %exchange.1 = (f32[64,264,128]{2,1,0:T(8,128)S(1)}, s32[8,256]{1,0:T(8,128)S(1)}) custom-call(s32[64,256]{1,0:T(8,128)} %index_ref.1, s32[8]{0:T(128)} %counts_hbm.1, bf16[8,2048,256]{2,1,0:T(8,128)(2,1)} %eff_hbm.1, f32[8,2048]{1,0:T(8,128)} %nom_hbm.1, s32[8,2048]{1,0:T(8,128)} %obs_hbm.1, f32[8,2048]{1,0:T(8,128)} %var_hbm.1, f32[64,1,128]{2,1,0:T(1,128)} %bitcast.2, ...), custom_call_target="tpu_custom_call" | custom-call | tf_op jit(solution)/shard_map/exchange/pallas_call | solution.py:610
  48.6 0.0 copy-done
  48.7 0.0 copy-done.1
  48.7 4.8 %fill.1 = (f32[8,512,512]{2,1,0:T(8,128)}, f32[2,1,128]{2,1,0:T(1,128)}) custom-call(s32[8,256]{1,0:T(8,128)S(1)} %get-tuple-element.6.plan_ref, f32[64,264,128]{2,1,0:T(8,128)S(1)} %get-tuple-element.7.payload_ref, s32[64,256]{1,0:T(8,128)S(1)} %copy-done, f32[64,1,128]{2,1,0:T(1,128)S(1)} %bitcast.3), custom_call_target="tpu_custom_call" | custom-call | tf_op jit(solution)/shard_map/fill/pallas_call | solution.py:728
Async XLA Ops:
  0.6 48.0 %copy-start = (s32[64,256]{1,0:T(8,128)S(1)}, s32[64,256]{1,0:T(8,128)}, u32[]{:S(2)}) copy-start(s32[64,256]{1,0:T(8,128)} %index_ref.1) | copy-start | bytes 196612
  0.6 48.0 %copy-start.1 = (f32[8192]{0:T(1024)S(1)}, f32[8192]{0:T(1024)}, u32[]{:S(2)}) copy-start(f32[8192]{0:T(1024)} %param.12) | copy-start | bytes 98308

commit v2 on v1

--- a/solution.py
+++ b/solution.py
@@ -234,8 +234,9 @@
     )(groups, tile_owner, payload, theta.reshape(-1, 1, GW))
 
 
-COLORS = ((0, 104, "zxy"), (104, 96, "zyx"), (200, 64, "xyz"))
+COLORS = ((0, 112, "zxy"), (112, 88, "zyx"), (200, 64, "xyz"))
 DEEP = 4
+TOGETHER = 4
 LINKS = 5
 
 
@@ -372,17 +373,14 @@
         (index_hbm, index_ref),
     ]
     smalls = [pltpu.make_async_copy(a, b, small_sem.at[n]) for n, (a, b) in enumerate(smalls)]
+    steps = [(q, h) for h in range(held) for q in range(4)]
     for made in smalls[:3]:
         made.start()
-    load(0, 0).start()
+    load(*steps[0]).start()
     for made in smalls[3:6]:
         made.start()
-    for h in range(held):
-        for q in range(4):
-            if (q, h) != (0, 0):
-                load(q, h).start()
-    for made in smalls[6:]:
-        made.start()
+    for step in steps[1:2]:
+        load(*step).start()
 
     partner = device(z, y, x, 1 - core)
     beside = device(z, y, 1 - x, core)
@@ -427,15 +425,24 @@
         parts_ref[at, GW : 2 * GW] = off
         parts_ref[at, 2 * GW :] = extra
 
-    steps = [(q, h) for h in range(held) for q in range(4)]
+    def begin(n):
+        load(*steps[n]).wait()
+        if n + 2 < len(steps):
+            load(*steps[n + 2]).start()
+        if n == 2:
+            for made in smalls[6:]:
+                made.start()
+        prepare(*steps[n])
 
     def compute(n):
         if n == 0:
-            load(*steps[0]).wait()
-            prepare(*steps[0])
+            begin(0)
+            multiply(*steps[0])
+            return
+        if n == 1:
+            begin(1)
         if n + 1 < len(steps):
-            load(*steps[n + 1]).wait()
-            prepare(*steps[n + 1])
+            begin(n + 1)
         multiply(*steps[n])
 
     def arrived(dst, sem):
@@ -556,41 +563,41 @@
 
 
 ORDER = (
-    (1, 0, 0, 0, 0), (1, 1, 0, 0, 0), (1, 2, 0, 0, 0), (0, 0, -1, 0, 0), (0, 0, 1, 0, 0),
-    (0, 1, -1, 0, 0), (1, 0, 1, 0, 0), (0, 1, 0, 0, 1), (1, 1, 1, 0, 0), (1, 0, -1, 0, 0),
-    (1, 1, -1, 0, 0), (0, 2, -1, 0, 0), (0, 2, 0, 1, 0), (0, 0, 2, 0, 0), (0, 0, 0, 0, 1),
-    (0, 0, 0, 1, 0), (1, 2, 0, 1, 0), (1, 0, -2, 0, 0), (0, 1, 1, 0, 0), (1, 2, 0, 0, 1),
-    (0, 0, 1, 0, 1), (1, 0, 2, 0, 0), (0, 0, -2, 0, 0), (0, 2, 0, 0, 1), (1, 2, -1, 1, 0),
-    (1, 0, 0, 1, 0), (0, 2, 1, 1, 0), (1, 1, 2, 0, 0), (1, 1, -2, 0, 0), (0, 2, 0, 1, 1),
-    (1, 0, -3, 0, 0), (0, 1, -2, 0, 0), (0, 1, 2, 0, 0), (0, 2, 1, 0, 0), (0, 1, -1, 0, 1),
-    (0, 0, -3, 0, 0), (1, 0, 3, 0, 0), (1, 0, 1, 0, 1), (1, 1, -3, 0, 0), (1, 0, -3, 1, 0),
-    (0, 2, -1, 1, 0), (0, 2, -1, 0, 1), (0, 2, 2, 1, 0), (1, 0, -1, 1, 0), (1, 2, 1, 0, 0),
-    (1, 1, 1, 0, 1), (1, 1, 3, 0, 0), (1, 2, -1, 0, 0), (0, 0, 2, 1, 0), (0, 1, 3, 0, 0),
-    (1, 1, 0, 0, 1), (1, 2, 0, 1, 1), (1, 0, -2, 1, 0), (0, 1, -3, 0, 0), (1, 2, 1, 0, 1),
-    (0, 0, 3, 0, 0), (1, 2, 1, 1, 0), (1, 1, 3, 1, 0), (0, 2, 1, 0, 1), (0, 0, -2, 0, 1),
-    (1, 2, -1, 0, 1), (1, 2, -2, 1, 0), (1, 1, -3, 0, 1), (1, 0, -1, 0, 1), (0, 2, 3, 1, 0),
-    (1, 0, 1, 1, 0), (0, 2, 2, 0, 0), (1, 0, -2, 0, 1), (1, 0, -3, 0, 1), (0, 1, 1, 0, 1),
-    (0, 2, -2, 0, 0), (0, 2, -1, 1, 1), (1, 0, 3, 1, 0), (0, 2, 1, 1, 1), (1, 1, -3, 1, 0),
-    (1, 1, 3, 0, 1), (0, 2, -2, 0, 1), (1, 0, 2, 1, 0), (1, 1, -2, 0, 1), (1, 0, 0, 1, 1),
-    (0, 1, -2, 0, 1), (1, 0, 3, 0, 1), (1, 2, -1, 1, 1), (0, 0, -2, 1, 0), (0, 1, 1, 1, 0),
-    (1, 1, 0, 1, 0), (0, 1, 3, 0, 1), (0, 0, -3, 1, 0), (1, 2, -2, 0, 0), (1, 2, 2, 0, 0),
-    (0, 1, 2, 0, 1), (0, 0, -1, 0, 1), (0, 2, 3, 0, 0), (1, 2, 1, 1, 1), (1, 2, 2, 0, 1),
-    (0, 0, 3, 1, 0), (1, 2, -2, 0, 1), (0, 1, -3, 1, 0), (0, 1, 2, 1, 0), (1, 1, 2, 0, 1),
-    (1, 1, -1, 0, 1), (0, 0, 1, 1, 0), (1, 1, -3, 1, 1), (0, 2, -2, 1, 0), (0, 2, 2, 0, 1),
-    (0, 0, 2, 0, 1), (0, 2, -2, 1, 1), (1, 1, 1, 1, 0), (1, 0, 2, 0, 1), (0, 1, 3, 1, 0),
-    (0, 1, 3, 1, 1), (0, 0, -1, 1, 0), (0, 1, -3, 0, 1), (1, 2, 2, 1, 0), (0, 0, -3, 1, 1),
-    (1, 2, -3, 1, 0), (0, 2, -3, 1, 0), (0, 1, 0, 1, 0), (0, 2, 3, 1, 1), (1, 2, 3, 0, 0),
-    (1, 2, -2, 1, 1), (0, 2, -3, 0, 0), (0, 0, -2, 1, 1), (0, 0, -3, 0, 1), (0, 1, 0, 1, 1),
-    (0, 0, 3, 1, 1), (0, 0, 3, 0, 1), (1, 0, 3, 1, 1), (1, 2, -3, 0, 0), (1, 0, -2, 1, 1),
-    (0, 0, 0, 1, 1), (0, 1, -1, 1, 0), (0, 1, -1, 1, 1), (1, 1, 0, 1, 1), (1, 0, -1, 1, 1),
-    (0, 1, -2, 1, 0), (1, 1, 1, 1, 1), (1, 2, 3, 0, 1), (0, 0, 2, 1, 1), (1, 0, 0, 0, 1),
-    (0, 2, 2, 1, 1), (0, 2, 3, 0, 1), (1, 2, 2, 1, 1), (1, 0, 1, 1, 1), (1, 1, -2, 1, 1),
-    (1, 1, 2, 1, 0), (0, 2, -3, 1, 1), (0, 0, 1, 1, 1), (0, 1, -2, 1, 1), (0, 1, 2, 1, 1),
-    (1, 0, -3, 1, 1), (1, 2, -3, 0, 1), (0, 2, -3, 0, 1), (0, 1, 1, 1, 1), (1, 1, -2, 1, 0),
-    (1, 1, -1, 1, 0), (1, 2, 3, 1, 0), (0, 0, -1, 1, 1), (1, 1, 2, 1, 1), (0, 1, -3, 1, 1),
-    (1, 0, 2, 1, 1), (1, 1, 3, 1, 1), (1, 2, 3, 1, 1), (1, 1, -1, 1, 1), (1, 2, -3, 1, 1),
+    (1, 0, 0, 0, 0), (1, 1, 0, 0, 0), (1, 2, 0, 0, 0), (0, 0, -1, 0, 0), (0, 2, 0, 0, 1),
+    (0, 0, 1, 0, 0), (1, 0, 1, 0, 0), (0, 1, 1, 0, 0), (1, 0, -1, 0, 0), (1, 1, 1, 0, 0),
+    (1, 1, -1, 0, 0), (0, 2, 0, 1, 0), (0, 1, -1, 0, 0), (0, 0, 0, 1, 0), (1, 2, 0, 1, 0),
+    (1, 0, 2, 0, 0), (1, 1, 0, 0, 1), (0, 1, 2, 0, 0), (1, 1, 2, 0, 0), (1, 1, -2, 0, 0),
+    (0, 2, -1, 0, 0), (0, 1, -2, 0, 0), (1, 0, 0, 0, 1), (1, 2, -1, 1, 0), (0, 2, 1, 0, 0),
+    (1, 0, -2, 0, 0), (1, 1, 0, 1, 0), (0, 0, 2, 0, 0), (1, 2, 1, 1, 0), (0, 1, 1, 0, 1),
+    (0, 0, 1, 1, 0), (1, 1, -3, 0, 0), (1, 0, 1, 0, 1), (0, 1, 3, 0, 0), (0, 0, -2, 0, 0),
+    (1, 0, 3, 0, 0), (1, 2, 0, 0, 1), (0, 2, 0, 1, 1), (1, 0, 0, 1, 0), (1, 2, 1, 0, 0),
+    (1, 2, 1, 0, 1), (1, 1, 1, 1, 0), (1, 0, -3, 0, 0), (1, 2, 0, 1, 1), (1, 2, 2, 1, 0),
+    (0, 0, -3, 0, 0), (0, 2, -1, 0, 1), (0, 2, -1, 1, 1), (0, 0, 3, 0, 0), (0, 1, 2, 0, 1),
+    (0, 1, -3, 0, 0), (0, 2, -2, 0, 0), (1, 2, -1, 0, 0), (1, 1, 3, 0, 0), (0, 1, -2, 0, 1),
+    (1, 0, -3, 1, 0), (0, 1, 0, 0, 1), (1, 0, 2, 1, 0), (0, 2, 1, 0, 1), (1, 1, 1, 0, 1),
+    (1, 0, -1, 1, 0), (0, 1, -3, 0, 1), (0, 0, -1, 1, 0), (0, 2, 1, 1, 1), (0, 2, 1, 1, 0),
+    (0, 0, 1, 0, 1), (1, 1, -1, 0, 1), (1, 0, 3, 1, 0), (1, 2, 1, 1, 1), (0, 2, -1, 1, 0),
+    (0, 1, 1, 1, 0), (0, 2, 2, 0, 0), (1, 2, 2, 0, 1), (0, 0, 3, 0, 1), (0, 0, -3, 1, 0),
+    (1, 2, 2, 0, 0), (1, 1, 2, 0, 1), (0, 0, 3, 1, 0), (1, 2, 3, 1, 0), (1, 2, -1, 0, 1),
+    (1, 0, -1, 0, 1), (0, 2, -2, 0, 1), (0, 0, -2, 0, 1), (1, 1, -3, 0, 1), (1, 2, -1, 1, 1),
+    (1, 0, 1, 1, 0), (1, 1, -2, 0, 1), (0, 0, 2, 1, 0), (1, 0, 3, 0, 1), (0, 2, -3, 0, 0),
+    (0, 0, -3, 0, 1), (0, 2, 2, 1, 1), (0, 0, -1, 0, 1), (1, 1, 3, 0, 1), (0, 1, -1, 0, 1),
+    (0, 2, -2, 1, 0), (0, 1, 2, 1, 0), (1, 0, -2, 1, 0), (1, 2, -2, 0, 1), (0, 2, 2, 0, 1),
+    (1, 2, 2, 1, 1), (0, 0, -2, 1, 0), (1, 1, 3, 1, 0), (1, 2, -2, 1, 0), (1, 0, -3, 1, 1),
+    (0, 1, 3, 0, 1), (1, 0, 0, 1, 1), (0, 2, -3, 1, 0), (1, 2, -2, 0, 0), (0, 2, -3, 0, 1),
+    (1, 2, -3, 1, 0), (1, 2, -3, 1, 1), (1, 1, 3, 1, 1), (1, 2, -2, 1, 1), (1, 0, 2, 1, 1),
+    (0, 1, 2, 1, 1), (0, 0, 1, 1, 1), (0, 2, 2, 1, 0), (0, 1, 0, 1, 1), (1, 1, 1, 1, 1),
+    (1, 1, 2, 1, 1), (1, 0, -2, 0, 1), (0, 1, 3, 1, 0), (0, 0, 0, 0, 1), (1, 1, -3, 1, 0),
+    (1, 1, 2, 1, 0), (1, 0, -3, 0, 1), (1, 1, -1, 1, 1), (0, 1, -2, 1, 1), (0, 2, 3, 0, 1),
+    (1, 1, -2, 1, 0), (1, 1, 0, 1, 1), (1, 2, 3, 0, 1), (0, 2, 3, 0, 0), (0, 0, 2, 0, 1),
+    (0, 1, 3, 1, 1), (0, 1, -1, 1, 0), (1, 2, -3, 0, 1), (1, 1, -3, 1, 1), (0, 0, -3, 1, 1),
+    (0, 1, -3, 1, 1), (0, 2, -3, 1, 1), (1, 1, -1, 1, 0), (0, 1, 1, 1, 1), (0, 2, -2, 1, 1),
+    (0, 0, 0, 1, 1), (1, 0, -1, 1, 1), (1, 0, 3, 1, 1), (0, 0, -1, 1, 1), (0, 0, 3, 1, 1),
+    (1, 2, 3, 1, 1), (0, 2, 3, 1, 1), (1, 1, -2, 1, 1), (1, 0, 2, 0, 1), (0, 1, -3, 1, 0),
+    (1, 2, 3, 0, 0), (0, 0, -2, 1, 1), (1, 0, 1, 1, 1), (0, 1, 0, 1, 0), (0, 0, 2, 1, 1),
+    (0, 1, -2, 1, 0), (1, 2, -3, 0, 0), (1, 0, -2, 1, 1), (0, 2, 3, 1, 0), (0, 1, -1, 1, 1),
 )
-PLAN_AT = 40
+PLAN_AT = 0
 
 
 def exchange(effects, nominal, observed, variance, theta, nuisance_index, counts, tile_owner):
@@ -645,63 +652,30 @@
     )(*[pltpu.with_memory_space_constraint(a, pltpu.HBM) for a in operands])
 
 
-def fill_kernel(plan_ref, payload_ref, index_ref, theta_ref, tiles_ref, grad_ref, held_tiles, sems):
+def fill_kernel(
+    plan_hbm, payload_ref, index_ref, theta_ref, tiles_ref, grad_hbm,
+    plan_ref, grad_ref, held_tiles, sems, small_sems,
+):
     slots = held_tiles.shape[0]
     per_tile = TILE // GW
     shift = per_tile.bit_length() - 1
     row = lax.broadcasted_iota(jnp.int32, (GW, GW), 0)
     col = lax.broadcasted_iota(jnp.int32, (GW, GW), 1)
     eye = (row == col).astype(jnp.float32)
+    ahead = min(2, slots)
+
+    get_plan = pltpu.make_async_copy(plan_hbm, plan_ref, small_sems.at[0])
+    put_grad = pltpu.make_async_copy(grad_ref, grad_hbm, small_sems.at[1])
+    get_plan.start()
 
     def put(s):
         return pltpu.make_async_copy(held_tiles.at[s], tiles_ref.at[s], sems.at[s])
 
-    def one_tile(s, _):
+    def clear(s):
         held_tiles[s] = jnp.zeros((TILE, TILE), jnp.float32)
 
-        @pl.when(plan_ref[2, s] == 1)
-        def _():
-            for r in range(per_tile):
-                held_tiles[s, r * GW : (r + 1) * GW, r * GW : (r + 1) * GW] = eye
-
-        def accumulate(i, _):
-            code = plan_ref[0, i]
-            kind = code & 3
-            rc = (code >> 2) & (per_tile - 1)
-            rr = (code >> (2 + shift)) & (per_tile - 1)
-            c = code >> (2 + 2 * shift)
-            at = (
-                s,
-                pl.ds(pl.multiple_of(rr * GW, GW), GW),
-                pl.ds(pl.multiple_of(rc * GW, GW), GW),
-            )
-
-            @pl.when(kind == 0)
-            def _():
-                block = payload_ref[c, :GW]
-                held_tiles[at] += jnp.where(row <= col, block, block.T)
-
-            @pl.when(kind == 1)
-            def _():
-                block = payload_ref[c, :GW]
-                diag = jnp.where(row == col, payload_ref[c, 2 * GW + 2 : 2 * GW + 3], block.T)
-                held_tiles[at] += jnp.where(row > col, block, diag)
-
-            @pl.when(kind == 2)
-            def _():
-                held_tiles[at] += payload_ref[c, GW : 2 * GW]
-
-            @pl.when(kind == 3)
-            def _():
-                held_tiles[at] += payload_ref[c, GW : 2 * GW].T
-
-            return 0
-
-        lax.fori_loop(plan_ref[1, s], plan_ref[1, s + 1], accumulate, 0)
-        put(s).start()
-        return 0
-
-    lax.fori_loop(0, slots, one_tile, 0)
+    for s in range(ahead):
+        clear(s)
 
     mine = grad_ref.shape[0]
     device = lax.axis_index("chan") * lax.axis_size("bins") + lax.axis_index("bins")
@@ -714,28 +688,78 @@
             hit = (index_ref[:, r * GW : (r + 1) * GW] >> gshift) == first + m
             acc += jnp.sum(jnp.where(hit, payload_ref[:, 2 * GW + r], 0.0), axis=0, keepdims=True)
         grad_ref[m] = acc
+    put_grad.start()
+    get_plan.wait()
+
+    def one_tile(s, _):
+        @pl.when(plan_ref[2, s] == 1)
+        def _():
+            for r in range(per_tile):
+                held_tiles[s, r * GW : (r + 1) * GW, r * GW : (r + 1) * GW] = eye
+
+        start, end = plan_ref[1, s], plan_ref[1, s + 1]
+
+        def block_of(i):
+            valid = i < end
+            code = plan_ref[0, jnp.minimum(i, end - 1)]
+            kind = code & 3
+            rc = (code >> 2) & (per_tile - 1)
+            rr = (code >> (2 + shift)) & (per_tile - 1)
+            c = code >> (2 + 2 * shift)
+            block = payload_ref[c, pl.ds(pl.multiple_of((kind >> 1) * GW, GW), GW)]
+            side = jnp.where(kind == 0, row - col, jnp.where(kind == 1, col - row, kind - 2))
+            value = jnp.where(side > 0, block.T, block)
+            diag = payload_ref[c, 2 * GW + 2 : 2 * GW + 3]
+            value = jnp.where(jnp.logical_and(kind == 1, row == col), diag, value)
+            at = (
+                s,
+                pl.ds(pl.multiple_of(rr * GW, GW), GW),
+                pl.ds(pl.multiple_of(rc * GW, GW), GW),
+            )
+            return at, jnp.where(valid, value, 0.0)
+
+        def accumulate(i, _):
+            for at, value in [block_of(start + i * TOGETHER + j) for j in range(TOGETHER)]:
+                held_tiles[at] += value
+            return 0
+
+        lax.fori_loop(0, (end - start + TOGETHER - 1) // TOGETHER, accumulate, 0)
+        put(s).start()
+
+        @pl.when(s + ahead < slots)
+        def _():
+            clear(s + ahead)
+
+        return 0
+
+    lax.fori_loop(0, slots, one_tile, 0)
 
     def drain(s, _):
         put(s).wait()
         return 0
 
     lax.fori_loop(0, slots, drain, 0)
+    put_grad.wait()
 
 
 def fill(payload, plan, theta, nuisance_index, slots, mine):
     chans, rows = payload.shape[:2]
     vmem = pl.BlockSpec(memory_space=pltpu.VMEM)
+    hbm = pl.BlockSpec(memory_space=pltpu.HBM)
     return pl.pallas_call(
         fill_kernel,
-        in_specs=[pl.BlockSpec(memory_space=pltpu.SMEM), vmem, vmem, vmem],
-        out_specs=[pl.BlockSpec(memory_space=pltpu.HBM), vmem],
+        in_specs=[vmem, vmem, vmem, vmem],
+        out_specs=[hbm, hbm],
         out_shape=[
             jax.ShapeDtypeStruct((slots, TILE, TILE), jnp.float32),
             jax.ShapeDtypeStruct((mine, 1, GW), jnp.float32),
         ],
         scratch_shapes=[
+            pltpu.SMEM(plan.shape, plan.dtype),
+            pltpu.VMEM((mine, 1, GW), jnp.float32),
             pltpu.VMEM((slots, TILE, TILE), jnp.float32),
             pltpu.SemaphoreType.DMA((slots,)),
+            pltpu.SemaphoreType.DMA((2,)),
         ],
         compiler_params=pltpu.CompilerParams(
             vmem_limit_bytes=4 * chans * (rows + EXTRA) * GW + 4 * slots * TILE * TILE + 4 * 2**20

time: 54.3 us -> 51.3 us (0.945); the launches traced: 53.5 us -> 51 us
  Pallas kernels: 52.8 us -> 50.3 us
    pallas_call x1, Pallas kernels: 48 us -> 46.1 us  [exchange(): pl.pallas_call(functools.partial(exchange_kernel, 2, slots), in_specs=[hb...]
    pallas_call x1, Pallas kernels: 4.8 us -> 4.26 us  [fill(): pl.pallas_call(fill_kernel, in_specs=[vmem, vmem, vmem, vmem], out_specs=...]
where the time goes in v2:
time: 51.3 us; the launch traced here: 51 us
  Pallas kernels  50.3 us (98%)
  between operations  0.67 us (1%)
    pallas_call x1, Pallas kernels, exchange(): pl.pallas_call(functools.partial(exchange_kernel, 2, slots), in_specs=[hb...  46.1 us
    pallas_call x1, Pallas kernels, fill(): pl.pallas_call(fill_kernel, in_specs=[vmem, vmem, vmem, vmem], out_specs=...  4.26 us

profile of v2, /device:TPU:1, one launch (start us, length us, event | category | flops | bytes accessed | tf_op | source)
XLA Modules:
  0.0 51.0 jit_solution(7424511640098519501)
XLA Ops:
  0.6 0.0 copy-start
  0.6 0.0 copy-start.1
  0.7 46.1 %exchange.1 = (f32[64,264,128]{2,1,0:T(8,128)S(1)}, s32[8,256]{1,0:T(8,128)S(1)}) custom-call(s32[64,256]{1,0:T(8,128)} %index_ref.1, s32[8]{0:T(128)} %counts_hbm.1, bf16[8,2048,256]{2,1,0:T(8,128)(2,1)} %eff_hbm.1, f32[8,2048]{1,0:T(8,128)} %nom_hbm.1, s32[8,2048]{1,0:T(8,128)} %obs_hbm.1, f32[8,2048]{1,0:T(8,128)} %var_hbm.1, f32[64,1,128]{2,1,0:T(1,128)} %bitcast.2, ...), custom_call_target="tpu_custom_call" | custom-call | tf_op jit(solution)/shard_map/exchange/pallas_call | solution.py:617
  46.7 0.0 copy-done
  46.8 0.0 copy-done.1
  46.8 4.3 %fill.1 = (f32[8,512,512]{2,1,0:T(8,128)}, f32[2,1,128]{2,1,0:T(1,128)}) custom-call(s32[8,256]{1,0:T(8,128)S(1)} %get-tuple-element.6.plan_hbm, f32[64,264,128]{2,1,0:T(8,128)S(1)} %get-tuple-element.7.payload_ref, s32[64,256]{1,0:T(8,128)S(1)} %copy-done, f32[64,1,128]{2,1,0:T(1,128)S(1)} %bitcast.3), custom_call_target="tpu_custom_call" | custom-call | tf_op jit(solution)/shard_map/fill/pallas_call | solution.py:749
Async XLA Ops:
  0.6 46.1 %copy-start = (s32[64,256]{1,0:T(8,128)S(1)}, s32[64,256]{1,0:T(8,128)}, u32[]{:S(2)}) copy-start(s32[64,256]{1,0:T(8,128)} %index_ref.1) | copy-start | bytes 196612
  0.6 46.1 %copy-start.1 = (f32[8192]{0:T(1024)S(1)}, f32[8192]{0:T(1024)}, u32[]{:S(2)}) copy-start(f32[8192]{0:T(1024)} %param.12) | copy-start | bytes 98308

commit v3 on v2

--- a/solution.py
+++ b/solution.py
@@ -236,23 +236,25 @@
 
 COLORS = ((0, 112, "zxy"), (112, 88, "zyx"), (200, 64, "xyz"))
 DEEP = 4
+PIECE = 512
 TOGETHER = 4
 LINKS = 5
 
 
-def exponent_rows(eff, chosen, nominal, observed, variance, live, left_ref):
-    eff_t = eff.T
+def exponent_rows(eff_ref, chosen, nominal, observed, variance, live, left_ref, start, piece):
+    at = slice(start, start + piece)
+    eff_t = eff_ref[at].T
     exponent = jnp.dot(chosen, eff_t, preferred_element_type=jnp.float32)[0:8]
-    expected = nominal * jnp.exp(exponent)
-    denominator = 1.0 + expected * variance
-    residual = jnp.where(live, (expected - observed) / denominator, 0.0)
-    weight = jnp.where(live, expected / denominator, 0.0)
-    left_ref[: 2 * GW] = (eff_t.astype(jnp.float32) * weight[0:1]).astype(jnp.bfloat16)
-    left_ref[2 * GW :] = jnp.concatenate([residual, residual], axis=0).astype(jnp.bfloat16)
-
-
-def block_rows(left, eff):
-    full = jnp.dot(left, eff, preferred_element_type=jnp.float32)
+    expected = nominal[:, at] * jnp.exp(exponent)
+    denominator = 1.0 + expected * variance[:, at]
+    here = live[:, at]
+    residual = jnp.where(here, (expected - observed[:, at]) / denominator, 0.0)
+    weight = jnp.where(here, expected / denominator, 0.0)
+    left_ref[: 2 * GW, at] = (eff_t.astype(jnp.float32) * weight[0:1]).astype(jnp.bfloat16)
+    left_ref[2 * GW :, at] = jnp.concatenate([residual, residual], axis=0).astype(jnp.bfloat16)
+
+
+def block_rows(full):
     first, off, second = full[:GW, :GW], full[:GW, GW:], full[GW : 2 * GW, GW:]
     row = lax.broadcasted_iota(jnp.int32, (GW, GW), 0)
     col = lax.broadcasted_iota(jnp.int32, (GW, GW), 1)
@@ -400,7 +402,9 @@
     for made in smalls[:6]:
         made.wait()
 
-    def prepare(q, h):
+    piece = min(PIECE, size)
+
+    def prepare(q, h, start):
         c = owners[q] * held + h
         g0 = local_index[c, 0] >> (GW.bit_length() - 1)
         g1 = local_index[c, GW] >> (GW.bit_length() - 1)
@@ -409,21 +413,16 @@
         line = pl.ds(c, 1)
         position = bins * size + lax.broadcasted_iota(jnp.int32, (8, size), 1)
         exponent_rows(
-            eff_held[q * held + h],
+            eff_held.at[q * held + h],
             chosen,
             nom_ref[line],
             obs_ref[line].astype(jnp.float32),
             var_ref[line],
             position < counts_ref[c],
             left.at[q % 2],
+            start,
+            piece,
         )
-
-    def multiply(q, h):
-        packed, off, extra = block_rows(left[q % 2], eff_held[q * held + h])
-        at = q * held + h
-        parts_ref[at, :GW] = packed
-        parts_ref[at, GW : 2 * GW] = off
-        parts_ref[at, 2 * GW :] = extra
 
     def begin(n):
         load(*steps[n]).wait()
@@ -432,18 +431,33 @@
         if n == 2:
             for made in smalls[6:]:
                 made.start()
-        prepare(*steps[n])
+
+    def run_stage(first, second):
+        if second is not None:
+            begin(second)
+        full = None
+        for start in range(0, size, piece):
+            if first is not None:
+                q, h = steps[first]
+                at = slice(start, start + piece)
+                part = jnp.dot(
+                    left[q % 2, :, at], eff_held[q * held + h, at],
+                    preferred_element_type=jnp.float32,
+                )
+                full = part if full is None else full + part
+            if second is not None:
+                prepare(*steps[second], start)
+        if first is not None:
+            packed, off, extra = block_rows(full)
+            parts_ref[q * held + h, :GW] = packed
+            parts_ref[q * held + h, GW : 2 * GW] = off
+            parts_ref[q * held + h, 2 * GW :] = extra
 
     def compute(n):
-        if n == 0:
-            begin(0)
-            multiply(*steps[0])
-            return
-        if n == 1:
-            begin(1)
-        if n + 1 < len(steps):
-            begin(n + 1)
-        multiply(*steps[n])
+        if n < 2:
+            run_stage(None, n)
+        later = n + 1 if 0 < n < len(steps) - 1 else None
+        run_stage(n, later)
 
     def arrived(dst, sem):
         pltpu.make_async_remote_copy(

time: 51.3 us -> 50.7 us (0.988)
  Pallas kernels: 50.3 us -> 49.6 us
    pallas_call x1, Pallas kernels: 46.1 us -> 45.4 us  [exchange(): pl.pallas_call(functools.partial(exchange_kernel, 2, slots), in_specs=[hb...]
where the time goes in v3:
time: 50.7 us; the launch traced here: 50.3 us
  Pallas kernels  49.6 us (98%)
  between operations  0.67 us (1%)
    pallas_call x1, Pallas kernels, exchange(): pl.pallas_call(functools.partial(exchange_kernel, 2, slots), in_specs=[hb...  45.4 us
    pallas_call x1, Pallas kernels, fill(): pl.pallas_call(fill_kernel, in_specs=[vmem, vmem, vmem, vmem], out_specs=...  4.21 us

profile of v3, /device:TPU:1, one launch (start us, length us, event | category | flops | bytes accessed | tf_op | source)
XLA Modules:
  0.0 50.3 jit_solution(15633451284757406488)
XLA Ops:
  0.6 0.0 copy-start
  0.6 0.0 copy-start.1
  0.7 45.4 %exchange.1 = (f32[64,264,128]{2,1,0:T(8,128)S(1)}, s32[8,256]{1,0:T(8,128)S(1)}) custom-call(s32[64,256]{1,0:T(8,128)} %index_ref.1, s32[8]{0:T(128)} %counts_hbm.1, bf16[8,2048,256]{2,1,0:T(8,128)(2,1)} %eff_hbm.1, f32[8,2048]{1,0:T(8,128)} %nom_hbm.1, s32[8,2048]{1,0:T(8,128)} %obs_hbm.1, f32[8,2048]{1,0:T(8,128)} %var_hbm.1, f32[64,1,128]{2,1,0:T(1,128)} %bitcast.2, ...), custom_call_target="tpu_custom_call" | custom-call | tf_op jit(solution)/shard_map/exchange/pallas_call | solution.py:631
  46.1 0.0 copy-done
  46.1 0.0 copy-done.1
  46.1 4.2 %fill.1 = (f32[8,512,512]{2,1,0:T(8,128)}, f32[2,1,128]{2,1,0:T(1,128)}) custom-call(s32[8,256]{1,0:T(8,128)S(1)} %get-tuple-element.6.plan_hbm, f32[64,264,128]{2,1,0:T(8,128)S(1)} %get-tuple-element.7.payload_ref, s32[64,256]{1,0:T(8,128)S(1)} %copy-done, f32[64,1,128]{2,1,0:T(1,128)S(1)} %bitcast.3), custom_call_target="tpu_custom_call" | custom-call | tf_op jit(solution)/shard_map/fill/pallas_call | solution.py:763
Async XLA Ops:
  0.6 45.5 %copy-start = (s32[64,256]{1,0:T(8,128)S(1)}, s32[64,256]{1,0:T(8,128)}, u32[]{:S(2)}) copy-start(s32[64,256]{1,0:T(8,128)} %index_ref.1) | copy-start | bytes 196612
  0.6 45.5 %copy-start.1 = (f32[8192]{0:T(1024)S(1)}, f32[8192]{0:T(1024)}, u32[]{:S(2)}) copy-start(f32[8192]{0:T(1024)} %param.12) | copy-start | bytes 98308
